TPU v7x, 32 devices: a whole 2x2x4 slice. The times are simulated.
32 devices in a mesh: groups: 1, section: 2 (over x), axial: 16 (over z, y, core).
Axes of the slice: x: 2, y: 2, z: 4, core: 2. Of those that a mesh axis runs over, the one named last changes fastest.
Arguments:
- pair_in: bfloat16 [4, 128, 128, 128], P('groups', 'axial'), may hold values from -6 to 6
- crop_mask: int32 [4, 128], P('groups'), may hold values 0 or 1
- proj_weights: bfloat16 [2, 5, 128, 128], P('section'), may hold values from -0.5 to 0.5
- out_weights: bfloat16 [2, 128, 128], P('section'), may hold values from -0.5 to 0.5
- up_weights: bfloat16 [2, 128, 512], P('section'), may hold values from -0.5 to 0.5
- down_weights: bfloat16 [2, 512, 128], P('section'), may hold values from -0.25 to 0.25
- norm_gains: bfloat16 [2, 3, 128], P('section'), may hold values from 0.099609375 to 1.8984375
Outputs:
- pair_out: bfloat16 [4, 128, 128, 128], P(('groups', 'section'), 'axial')
Inputs may be any that keep to these rules, and one draw needn't show every extreme that they name: `crop_mask`: 1 marks a residue inside the crop, 0 a padded one.
All inputs are finite; a program needn't handle non-finite values.
Results may differ from a plain program's by a relative error of at most 0.013.
Values may be sent and summed in bfloat16 or wider, within the bound.
A program may use at most 64 MiB of HBM per device.

v0:
```python
import jax
import jax.numpy as jnp
from jax import lax
from jax.sharding import PartitionSpec as P

epsilon = 1e-05


def normalize(values, axis_dim):
    center = values - jnp.mean(values, axis=axis_dim, keepdims=True)
    spread = jnp.mean(center * center, axis=axis_dim, keepdims=True)
    return center * lax.rsqrt(spread + epsilon)


def triangle(pieces):
    return jnp.einsum(
        "gcik,gcjk->gcij", pieces[0], pieces[1], preferred_element_type=jnp.float32
    ).astype(jnp.bfloat16)


def evo_block(current, mask_all, proj_mats, out_mat, up_mat, down_mat, gain_rows):
    row_count = current.shape[0]
    width = current.shape[1]
    channels = current.shape[2]
    group_count = lax.axis_size("axial")
    per_group = channels // group_count
    row_start = lax.axis_index("axial") * row_count
    mask_rows = lax.dynamic_slice_in_dim(mask_all, row_start, row_count)
    gain_vals = gain_rows.astype(jnp.float32)
    pair_f = current.astype(jnp.float32)
    normed = (normalize(pair_f, 2) * gain_vals[0]).astype(jnp.bfloat16)
    linear = jnp.einsum("rnd,edc->ecrn", normed, proj_mats[:4], preferred_element_type=jnp.float32)
    pair_mask = mask_rows[:, None] * mask_all[None, :]
    left_edge = (jax.nn.sigmoid(linear[1]) * linear[0] * pair_mask).astype(jnp.bfloat16)
    right_edge = (jax.nn.sigmoid(linear[3]) * linear[2] * pair_mask).astype(jnp.bfloat16)
    left_groups = left_edge.reshape(group_count, per_group, row_count, width)
    right_groups = right_edge.reshape(group_count, per_group, row_count, width)
    product = triangle(
        (
            lax.all_to_all(left_groups, "axial", split_axis=0, concat_axis=2, tiled=True),
            lax.all_to_all(right_groups, "axial", split_axis=0, concat_axis=2, tiled=True),
        )
    )
    restored = lax.all_to_all(product, "axial", split_axis=2, concat_axis=0, tiled=True).reshape(
        channels, row_count, width
    )
    tri_norm = (normalize(restored.astype(jnp.float32), 0) * gain_vals[1][:, None, None]).astype(
        jnp.bfloat16
    )
    update = jnp.einsum("crn,cd->rnd", tri_norm, out_mat, preferred_element_type=jnp.float32)
    gate_values = jax.nn.sigmoid(
        jnp.einsum("rnd,dc->rnc", normed, proj_mats[4], preferred_element_type=jnp.float32)
    )
    pair_mid = pair_f + gate_values * update
    trans_in = (normalize(pair_mid, 2) * gain_vals[2]).astype(jnp.bfloat16).reshape(-1, channels)
    hidden = jax.nn.relu(jnp.dot(trans_in, up_mat, preferred_element_type=jnp.float32)).astype(
        jnp.bfloat16
    )
    pair_new = pair_mid + jnp.dot(hidden, down_mat, preferred_element_type=jnp.float32).reshape(
        pair_mid.shape
    )
    return pair_new.astype(jnp.bfloat16)


def per_device(pair_in, crop_mask, proj_weights, out_weights, up_weights, down_weights, norm_gains):
    section_index = lax.axis_index("section")
    section_count = lax.axis_size("section")
    micro_count = pair_in.shape[0]
    own_count = micro_count // section_count
    gathered = (
        lax.all_gather(proj_weights, "section", axis=0, tiled=True),
        lax.all_gather(out_weights, "section", axis=0, tiled=True),
        lax.all_gather(up_weights, "section", axis=0, tiled=True),
        lax.all_gather(down_weights, "section", axis=0, tiled=True),
        lax.all_gather(norm_gains, "section", axis=0, tiled=True),
    )
    own_pairs = lax.dynamic_slice_in_dim(pair_in, section_index * own_count, own_count, 0)
    own_masks = lax.dynamic_slice_in_dim(crop_mask, section_index * own_count, own_count, 0).astype(
        jnp.float32
    )
    outputs = []
    for member in range(own_count):
        current = own_pairs[member]
        for layer_index in range(section_count):
            current = evo_block(
                current,
                own_masks[member],
                gathered[0][layer_index],
                gathered[1][layer_index],
                gathered[2][layer_index],
                gathered[3][layer_index],
                gathered[4][layer_index],
            )
        outputs.append(current)
    return jnp.stack(outputs)


def solution(mesh):
    return jax.shard_map(
        per_device,
        mesh=mesh,
        in_specs=(
            P("groups", "axial", None, None),
            P("groups", None),
            P("section", None, None, None),
            P("section", None, None),
            P("section", None, None),
            P("section", None, None),
            P("section", None, None),
        ),
        out_specs=P(("groups", "section"), "axial", None, None),
        check_vma=False,
    )
```

profile of v0, /device:TPU:2, one launch (start us, length us, event | category | flops | bytes accessed | tf_op | source)
XLA Modules:
  0.0 205.5 jit_solution(10994964852828261965)
XLA Ops:
  2.9 4.5 %all_gather.15 = bf16[2,3,128]{2,1,0:T(4,128)(2,1)S(1)} all-gather(bf16[1,3,128]{2,1,0:T(4,128)(2,1)} %param.13), channel_id=1, replica_groups=mesh['groups'=1,'section'=2,'axial'=16] {'section'}, dimensions={0}, use_global_device_ids=true | all-gather | bytes 2304 | tf_op jit(solution)/shard_map/all_gather | solution.py:75
  7.4 6.2 %all_gather.16 = bf16[2,5,128,128]{3,2,1,0:T(8,128)(2,1)S(1)} all-gather(bf16[1,5,128,128]{3,2,1,0:T(8,128)(2,1)} %param.9), channel_id=1, replica_groups=mesh['groups'=1,'section'=2,'axial'=16] {'section'}, dimensions={0}, use_global_device_ids=true | all-gather | bytes 491520 | tf_op jit(solution)/shard_map/all_gather | solution.py:71
  18.3 6.0 %all-to-all-start.6 = ((bf16[16,8,8,128]{3,1,2,0:T(8,128)(2,1)}), bf16[16,8,8,128]{3,1,2,0:T(8,128)(2,1)}, u32[]{:S(2)}, u32[]{:S(2)}) async-start(bf16[16,8,8,128]{3,1,2,0:T(8,128)(2,1)} %get-tuple-element.27), calls=%async_computation.6 | async-start | bytes 524288 | tf_op jit(solution)/shard_map/all_to_all | solution.py:40
  25.0 9.3 %all-to-all-done.6 = bf16[16,8,8,128]{3,1,2,0:T(8,128)(2,1)} async-done(((bf16[16,8,8,128]{3,1,2,0:T(8,128)(2,1)}), bf16[16,8,8,128]{3,1,2,0:T(8,128)(2,1)}, u32[]{:S(2)}, u32[]{:S(2)}) %all-to-all-start.6) | async-done | bytes 262176 | tf_op jit(solution)/shard_map/all_to_all | solution.py:40
  34.4 4.2 %all-to-all-start.7 = ((bf16[16,8,8,128]{3,1,2,0:T(8,128)(2,1)}), bf16[16,8,8,128]{3,1,2,0:T(8,128)(2,1)}, u32[]{:S(2)}, u32[]{:S(2)}) async-start(bf16[16,8,8,128]{3,1,2,0:T(8,128)(2,1)} %get-tuple-element.28), calls=%async_computation.7 | async-start | bytes 524288 | tf_op jit(solution)/shard_map/all_to_all | solution.py:41
  39.8 8.8 %all-to-all-done.7 = bf16[16,8,8,128]{3,1,2,0:T(8,128)(2,1)} async-done(((bf16[16,8,8,128]{3,1,2,0:T(8,128)(2,1)}), bf16[16,8,8,128]{3,1,2,0:T(8,128)(2,1)}, u32[]{:S(2)}, u32[]{:S(2)}) %all-to-all-start.7) | async-done | bytes 262176 | tf_op jit(solution)/shard_map/all_to_all | solution.py:41
  48.6 12.7 %all_to_all.156 = bf16[16,8,8,128]{3,1,2,0:T(8,128)(2,1)S(1)} all-to-all(bf16[16,8,8,128]{3,1,2,0:T(8,128)(2,1)S(1)} %get-tuple-element.23), channel_id=1, replica_groups=mesh['groups'=1,'section'=2,'axial'=16] {'axial'}, dimensions={0} | all-to-all | bytes 524288 | tf_op jit(solution)/shard_map/all_to_all | solution.py:40
  61.3 3.5 %all-to-all-start.1 = ((bf16[16,8,8,128]{3,1,2,0:T(8,128)(2,1)}), bf16[16,8,8,128]{3,1,2,0:T(8,128)(2,1)S(1)}, u32[]{:S(2)}, u32[]{:S(2)}) async-start(bf16[16,8,8,128]{3,1,2,0:T(8,128)(2,1)} %get-tuple-element.24), calls=%async_computation.1 | async-start | bytes 524288 | tf_op jit(solution)/shard_map/all_to_all | solution.py:41
  65.0 4.6 %all_gather.17 = bf16[2,128,128]{2,1,0:T(8,128)(2,1)S(1)} all-gather(bf16[1,128,128]{2,1,0:T(8,128)(2,1)S(1)} %copy-done.7), channel_id=1, replica_groups=mesh['groups'=1,'section'=2,'axial'=16] {'section'}, dimensions={0}, use_global_device_ids=true | all-gather | bytes 98304 | tf_op jit(solution)/shard_map/all_gather | solution.py:72
  74.8 4.3 %all-to-all-start.8 = ((bf16[1,8,128,128]{3,1,0,2:T(8,128)(2,1)}), bf16[1,8,128,128]{3,1,0,2:T(8,128)(2,1)S(1)}, u32[]{:S(2)}, u32[]{:S(2)}) async-start(bf16[1,8,128,128]{3,1,0,2:T(8,128)(2,1)} %copy.96), calls=%async_computation.8 | async-start | bytes 524288 | tf_op jit(solution)/shard_map/all_to_all | solution.py:44
  79.1 6.5 %all_gather.18 = bf16[2,128,512]{2,1,0:T(8,128)(2,1)S(1)} all-gather(bf16[1,128,512]{2,1,0:T(8,128)(2,1)S(1)} %copy-done.5), channel_id=1, replica_groups=mesh['groups'=1,'section'=2,'axial'=16] {'section'}, dimensions={0}, use_global_device_ids=true | all-gather | bytes 393216 | tf_op jit(solution)/shard_map/all_gather | solution.py:73
  85.6 5.6 %all_gather.19 = bf16[2,512,128]{2,1,0:T(8,128)(2,1)S(1)} all-gather(bf16[1,512,128]{2,1,0:T(8,128)(2,1)S(1)} %copy-done.6), channel_id=1, replica_groups=mesh['groups'=1,'section'=2,'axial'=16] {'section'}, dimensions={0}, use_global_device_ids=true | all-gather | bytes 393216 | tf_op jit(solution)/shard_map/all_gather | solution.py:74
  94.4 5.7 %all-to-all-start.2 = ((bf16[1,8,128,128]{3,1,0,2:T(8,128)(2,1)}), bf16[1,8,128,128]{3,1,0,2:T(8,128)(2,1)S(1)}, u32[]{:S(2)}, u32[]{:S(2)}) async-start(bf16[1,8,128,128]{3,1,0,2:T(8,128)(2,1)} %copy.77), calls=%async_computation.2 | async-start | bytes 524288 | tf_op jit(solution)/shard_map/all_to_all | solution.py:44
  100.4 9.7 %all-to-all-done.2 = bf16[1,8,128,128]{3,1,0,2:T(8,128)(2,1)S(1)} async-done(((bf16[1,8,128,128]{3,1,0,2:T(8,128)(2,1)}), bf16[1,8,128,128]{3,1,0,2:T(8,128)(2,1)S(1)}, u32[]{:S(2)}, u32[]{:S(2)}) %all-to-all-start.2) | async-done | bytes 262176 | tf_op jit(solution)/shard_map/all_to_all | solution.py:44
  118.3 4.4 %all-to-all-start.9 = ((bf16[16,8,8,128]{3,1,2,0:T(8,128)(2,1)}), bf16[16,8,8,128]{3,1,2,0:T(8,128)(2,1)}, u32[]{:S(2)}, u32[]{:S(2)}) async-start(bf16[16,8,8,128]{3,1,2,0:T(8,128)(2,1)} %get-tuple-element.25), calls=%async_computation.9 | async-start | bytes 524288 | tf_op jit(solution)/shard_map/all_to_all | solution.py:40
  125.6 6.9 %all-to-all-done.9 = bf16[16,8,8,128]{3,1,2,0:T(8,128)(2,1)} async-done(((bf16[16,8,8,128]{3,1,2,0:T(8,128)(2,1)}), bf16[16,8,8,128]{3,1,2,0:T(8,128)(2,1)}, u32[]{:S(2)}, u32[]{:S(2)}) %all-to-all-start.9) | async-done | bytes 262176 | tf_op jit(solution)/shard_map/all_to_all | solution.py:40
  132.5 4.2 %all-to-all-start.10 = ((bf16[16,8,8,128]{3,1,2,0:T(8,128)(2,1)}), bf16[16,8,8,128]{3,1,2,0:T(8,128)(2,1)}, u32[]{:S(2)}, u32[]{:S(2)}) async-start(bf16[16,8,8,128]{3,1,2,0:T(8,128)(2,1)} %get-tuple-element.26), calls=%async_computation.10 | async-start | bytes 524288 | tf_op jit(solution)/shard_map/all_to_all | solution.py:41
  137.9 8.9 %all-to-all-done.10 = bf16[16,8,8,128]{3,1,2,0:T(8,128)(2,1)} async-done(((bf16[16,8,8,128]{3,1,2,0:T(8,128)(2,1)}), bf16[16,8,8,128]{3,1,2,0:T(8,128)(2,1)}, u32[]{:S(2)}, u32[]{:S(2)}) %all-to-all-start.10) | async-done | bytes 262176 | tf_op jit(solution)/shard_map/all_to_all | solution.py:41
  146.7 12.7 %all_to_all.157 = bf16[16,8,8,128]{3,1,2,0:T(8,128)(2,1)S(1)} all-to-all(bf16[16,8,8,128]{3,1,2,0:T(8,128)(2,1)S(1)} %get-tuple-element.19), channel_id=1, replica_groups=mesh['groups'=1,'section'=2,'axial'=16] {'axial'}, dimensions={0} | all-to-all | bytes 524288 | tf_op jit(solution)/shard_map/all_to_all | solution.py:40
  159.4 3.5 %all-to-all-start.4 = ((bf16[16,8,8,128]{3,1,2,0:T(8,128)(2,1)}), bf16[16,8,8,128]{3,1,2,0:T(8,128)(2,1)S(1)}, u32[]{:S(2)}, u32[]{:S(2)}) async-start(bf16[16,8,8,128]{3,1,2,0:T(8,128)(2,1)} %get-tuple-element.20), calls=%async_computation.4 | async-start | bytes 524288 | tf_op jit(solution)/shard_map/all_to_all | solution.py:41
  165.4 7.6 %all-to-all-done.4 = bf16[16,8,8,128]{3,1,2,0:T(8,128)(2,1)S(1)} async-done(((bf16[16,8,8,128]{3,1,2,0:T(8,128)(2,1)}), bf16[16,8,8,128]{3,1,2,0:T(8,128)(2,1)S(1)}, u32[]{:S(2)}, u32[]{:S(2)}) %all-to-all-start.4) | async-done | bytes 262176 | tf_op jit(solution)/shard_map/all_to_all | solution.py:41
  180.2 6.3 %all-to-all-done.11 = bf16[1,8,128,128]{3,1,0,2:T(8,128)(2,1)S(1)} async-done(((bf16[1,8,128,128]{3,1,0,2:T(8,128)(2,1)}), bf16[1,8,128,128]{3,1,0,2:T(8,128)(2,1)S(1)}, u32[]{:S(2)}, u32[]{:S(2)}) %all-to-all-start.11) | async-done | bytes 262176 | tf_op jit(solution)/shard_map/all_to_all | solution.py:44
  186.5 3.5 %all-to-all-start.5 = ((bf16[1,8,128,128]{3,1,0,2:T(8,128)(2,1)}), bf16[1,8,128,128]{3,1,0,2:T(8,128)(2,1)S(1)}, u32[]{:S(2)}, u32[]{:S(2)}) async-start(bf16[1,8,128,128]{3,1,0,2:T(8,128)(2,1)} %copy.87), calls=%async_computation.5 | async-start | bytes 524288 | tf_op jit(solution)/shard_map/all_to_all | solution.py:44
  190.3 9.7 %all-to-all-done.5 = bf16[1,8,128,128]{3,1,0,2:T(8,128)(2,1)S(1)} async-done(((bf16[1,8,128,128]{3,1,0,2:T(8,128)(2,1)}), bf16[1,8,128,128]{3,1,0,2:T(8,128)(2,1)S(1)}, u32[]{:S(2)}, u32[]{:S(2)}) %all-to-all-start.5) | async-done | bytes 262176 | tf_op jit(solution)/shard_map/all_to_all | solution.py:44
  (136 shorter events, 45.5 us)
Async XLA Ops:
  2.9 13.8 %copy-start.8 = (f32[8,128]{1,0:T(8,128)}, f32[8,128]{1,0:T(8,128)S(1)}, u32[]{:S(2)}) copy-start(f32[8,128]{1,0:T(8,128)S(1)} %add_rsqrt_fusion.5) | copy-start | bytes 12292
  13.6 56.0 %copy-start.3 = (bf16[2,5,128,128]{3,2,1,0:T(8,128)(2,1)}, bf16[2,5,128,128]{3,2,1,0:T(8,128)(2,1)S(1)}, u32[]{:S(2)}) copy-start(bf16[2,5,128,128]{3,2,1,0:T(8,128)(2,1)S(1)} %all_gather.16) | copy-start | bytes 983044
  14.8 9.5 %copy-start.13 = (f32[128]{0:T(128)}, f32[128]{0:T(128)S(1)}, u32[]{:S(2)}) copy-start(f32[128]{0:T(128)S(1)} %get-tuple-element.59) | copy-start | bytes 1540
  16.5 7.9 %copy-start = (bf16[4,8,128,128]{3,2,1,0:T(8,128)(2,1)S(1)}, bf16[4,8,128,128]{3,2,1,0:T(8,128)(2,1)}, u32[]{:S(2)}) copy-start(bf16[4,8,128,128]{3,2,1,0:T(8,128)(2,1)} %param.7) | copy-start | bytes 3145732
  18.3 16.1 %all-to-all-start.6 = ((bf16[16,8,8,128]{3,1,2,0:T(8,128)(2,1)}), bf16[16,8,8,128]{3,1,2,0:T(8,128)(2,1)}, u32[]{:S(2)}, u32[]{:S(2)}) async-start(bf16[16,8,8,128]{3,1,2,0:T(8,128)(2,1)} %get-tuple-element.27), calls=%async_computation.6 | async-start | bytes 524288 | tf_op jit(solution)/shard_map/all_to_all | solution.py:40
  24.3 14.5 %copy-start.10 = (f32[8,128]{1,0:T(8,128)}, f32[8,128]{1,0:T(8,128)S(1)}, u32[]{:S(2)}) copy-start(f32[8,128]{1,0:T(8,128)S(1)} %add_rsqrt_fusion.11) | copy-start | bytes 12292
  34.4 14.2 %all-to-all-start.7 = ((bf16[16,8,8,128]{3,1,2,0:T(8,128)(2,1)}), bf16[16,8,8,128]{3,1,2,0:T(8,128)(2,1)}, u32[]{:S(2)}, u32[]{:S(2)}) async-start(bf16[16,8,8,128]{3,1,2,0:T(8,128)(2,1)} %get-tuple-element.28), calls=%async_computation.7 | async-start | bytes 524288 | tf_op jit(solution)/shard_map/all_to_all | solution.py:41
  38.9 26.1 %copy-start.7 = (bf16[1,128,128]{2,1,0:T(8,128)(2,1)S(1)}, bf16[1,128,128]{2,1,0:T(8,128)(2,1)}, u32[]{:S(2)}) copy-start(bf16[1,128,128]{2,1,0:T(8,128)(2,1)} %param.10) | copy-start | bytes 98308
  38.9 30.7 %copy-start.9 = (f32[8,128]{1,0:T(8,128)S(1)}, f32[8,128]{1,0:T(8,128)}, u32[]{:S(2)}) copy-start(f32[8,128]{1,0:T(8,128)} %copy-done.8) | copy-start | bytes 12292
  38.9 30.7 %copy-start.14 = (f32[128]{0:T(128)S(1)}, f32[128]{0:T(128)}, u32[]{:S(2)}) copy-start(f32[128]{0:T(128)} %copy-done.13) | copy-start | bytes 1540
  61.3 13.5 %all-to-all-start.1 = ((bf16[16,8,8,128]{3,1,2,0:T(8,128)(2,1)}), bf16[16,8,8,128]{3,1,2,0:T(8,128)(2,1)S(1)}, u32[]{:S(2)}, u32[]{:S(2)}) async-start(bf16[16,8,8,128]{3,1,2,0:T(8,128)(2,1)} %get-tuple-element.24), calls=%async_computation.1 | async-start | bytes 524288 | tf_op jit(solution)/shard_map/all_to_all | solution.py:41
  69.6 9.5 %copy-start.5 = (bf16[1,128,512]{2,1,0:T(8,128)(2,1)S(1)}, bf16[1,128,512]{2,1,0:T(8,128)(2,1)}, u32[]{:S(2)}) copy-start(bf16[1,128,512]{2,1,0:T(8,128)(2,1)} %param.11) | copy-start | bytes 393220
  69.6 16.0 %copy-start.6 = (bf16[1,512,128]{2,1,0:T(8,128)(2,1)S(1)}, bf16[1,512,128]{2,1,0:T(8,128)(2,1)}, u32[]{:S(2)}) copy-start(bf16[1,512,128]{2,1,0:T(8,128)(2,1)} %param.12) | copy-start | bytes 393220
  69.6 21.6 %copy-start.11 = (f32[8,128]{1,0:T(8,128)S(1)}, f32[8,128]{1,0:T(8,128)}, u32[]{:S(2)}) copy-start(f32[8,128]{1,0:T(8,128)} %copy-done.10) | copy-start | bytes 12292
  74.8 19.6 %all-to-all-start.8 = ((bf16[1,8,128,128]{3,1,0,2:T(8,128)(2,1)}), bf16[1,8,128,128]{3,1,0,2:T(8,128)(2,1)S(1)}, u32[]{:S(2)}, u32[]{:S(2)}) async-start(bf16[1,8,128,128]{3,1,0,2:T(8,128)(2,1)} %copy.96), calls=%async_computation.8 | async-start | bytes 524288 | tf_op jit(solution)/shard_map/all_to_all | solution.py:44
  85.6 37.1 %copy-start.1 = (bf16[2,128,512]{2,1,0:T(8,128)(2,1)}, bf16[2,128,512]{2,1,0:T(8,128)(2,1)S(1)}, u32[]{:S(2)}) copy-start(bf16[2,128,512]{2,1,0:T(8,128)(2,1)S(1)} %all_gather.18) | copy-start | bytes 786436
  94.4 15.7 %all-to-all-start.2 = ((bf16[1,8,128,128]{3,1,0,2:T(8,128)(2,1)}), bf16[1,8,128,128]{3,1,0,2:T(8,128)(2,1)S(1)}, u32[]{:S(2)}, u32[]{:S(2)}) async-start(bf16[1,8,128,128]{3,1,0,2:T(8,128)(2,1)} %copy.77), calls=%async_computation.2 | async-start | bytes 524288 | tf_op jit(solution)/shard_map/all_to_all | solution.py:44
  110.8 2.8 %copy-start.16 = (f32[128]{0:T(128)S(1)}, f32[128]{0:T(128)}, u32[]{:S(2)}) copy-start(f32[128]{0:T(128)} %get-tuple-element.61) | copy-start | bytes 1540
  118.3 14.2 %all-to-all-start.9 = ((bf16[16,8,8,128]{3,1,2,0:T(8,128)(2,1)}), bf16[16,8,8,128]{3,1,2,0:T(8,128)(2,1)}, u32[]{:S(2)}, u32[]{:S(2)}) async-start(bf16[16,8,8,128]{3,1,2,0:T(8,128)(2,1)} %get-tuple-element.25), calls=%async_computation.9 | async-start | bytes 524288 | tf_op jit(solution)/shard_map/all_to_all | solution.py:40
  132.5 14.2 %all-to-all-start.10 = ((bf16[16,8,8,128]{3,1,2,0:T(8,128)(2,1)}), bf16[16,8,8,128]{3,1,2,0:T(8,128)(2,1)}, u32[]{:S(2)}, u32[]{:S(2)}) async-start(bf16[16,8,8,128]{3,1,2,0:T(8,128)(2,1)} %get-tuple-element.26), calls=%async_computation.10 | async-start | bytes 524288 | tf_op jit(solution)/shard_map/all_to_all | solution.py:41
  137.0 26.0 %copy-start.17 = (f32[128]{0:T(128)S(1)}, f32[128]{0:T(128)}, u32[]{:S(2)}) copy-start(f32[128]{0:T(128)} %get-tuple-element.30) | copy-start | bytes 1540
  159.4 13.5 %all-to-all-start.4 = ((bf16[16,8,8,128]{3,1,2,0:T(8,128)(2,1)}), bf16[16,8,8,128]{3,1,2,0:T(8,128)(2,1)S(1)}, u32[]{:S(2)}, u32[]{:S(2)}) async-start(bf16[16,8,8,128]{3,1,2,0:T(8,128)(2,1)} %get-tuple-element.20), calls=%async_computation.4 | async-start | bytes 524288 | tf_op jit(solution)/shard_map/all_to_all | solution.py:41
  173.0 13.5 %all-to-all-start.11 = ((bf16[1,8,128,128]{3,1,0,2:T(8,128)(2,1)}), bf16[1,8,128,128]{3,1,0,2:T(8,128)(2,1)S(1)}, u32[]{:S(2)}, u32[]{:S(2)}) async-start(bf16[1,8,128,128]{3,1,0,2:T(8,128)(2,1)} %copy.104), calls=%async_computation.11 | async-start | bytes 524288 | tf_op jit(solution)/shard_map/all_to_all | solution.py:44
  186.5 13.5 %all-to-all-start.5 = ((bf16[1,8,128,128]{3,1,0,2:T(8,128)(2,1)}), bf16[1,8,128,128]{3,1,0,2:T(8,128)(2,1)S(1)}, u32[]{:S(2)}, u32[]{:S(2)}) async-start(bf16[1,8,128,128]{3,1,0,2:T(8,128)(2,1)} %copy.87), calls=%async_computation.5 | async-start | bytes 524288 | tf_op jit(solution)/shard_map/all_to_all | solution.py:44
  (5 other events, 7.0 us)
where the time goes:
time: 209 us; the launch traced here: 206 us
  waiting for transfers between devices  69 us (33%)
  blocking collectives  52.7 us (25%)
  starting transfers between devices  42.8 us (20%)
  matrix products  20.7 us (10%)
  other arithmetic  13.6 us (7%)
  local copies, waits for them, and re-layouts  5.9 us (3%)
    all_to_all x4, waiting for transfers between devices, evo_block(): lax.all_to_all(right_groups, 'axial', split_axis=0, concat_axis=2, tiled=...  27.1 us
    all_to_all x4, waiting for transfers between devices, evo_block(): lax.all_to_all(product, 'axial', split_axis=2, concat_axis=0, tiled=True)  25.7 us
    all_to_all x2, blocking collectives, evo_block(): lax.all_to_all(left_groups, 'axial', split_axis=0, concat_axis=2, tiled=T...  25.4 us
    all_to_all x4, starting transfers between devices, evo_block(): lax.all_to_all(product, 'axial', split_axis=2, concat_axis=0, tiled=True)  17 us
    all_to_all x2, waiting for transfers between devices, evo_block(): lax.all_to_all(left_groups, 'axial', split_axis=0, concat_axis=2, tiled=T...  16.3 us
    all_to_all x4, starting transfers between devices, evo_block(): lax.all_to_all(right_groups, 'axial', split_axis=0, concat_axis=2, tiled=...  15.4 us
    all_to_all x2, starting transfers between devices, evo_block(): lax.all_to_all(left_groups, 'axial', split_axis=0, concat_axis=2, tiled=T...  10.4 us
    all_gather x1, blocking collectives, per_device(): lax.all_gather(up_weights, 'section', axis=0, tiled=True)  6.47 us
  transfers between devices with their start and end apart: 10, of which 9 were waited for; matrix products, arithmetic and copies ran while one was open for 9% of the time, Pallas kernels for 0%

commit v1 on v0

--- a/solution.py
+++ b/solution.py
@@ -1,6 +1,10 @@
+import functools
+
 import jax
 import jax.numpy as jnp
 from jax import lax
+from jax.experimental import pallas as pl
+from jax.experimental.pallas import tpu as pltpu
 from jax.sharding import PartitionSpec as P
 
 epsilon = 1e-05
@@ -62,7 +66,396 @@
     return pair_new.astype(jnp.bfloat16)
 
 
+MESH = pl.DeviceIdType.MESH
+
+
+def sigmoid(values):
+    return 0.5 * jnp.tanh(0.5 * values) + 0.5
+
+
+def normalize_rows(values, gain):
+    scale = 1.0 / values.shape[0]
+    center = values - jnp.sum(values, axis=0, keepdims=True) * scale
+    spread = jnp.sum(center * center, axis=0, keepdims=True) * scale
+    return center * lax.rsqrt(spread + epsilon) * gain
+
+
+def matmul(mat, values):
+    return lax.dot_general(mat, values, (((1,), (0,)), ((), ())), preferred_element_type=jnp.float32)
+
+
+def fused_kernel(
+    sections,
+    peers,
+    own_count,
+    sub_rows,
+    pair_ref,
+    mask_ref,
+    mask_smem,
+    proj_ref,
+    out_ref,
+    up_ref,
+    down_ref,
+    gain_ref,
+    result_ref,
+    pair_buf,
+    z_buf,
+    normed_buf,
+    gate_buf,
+    edge_send,
+    edge_recv,
+    tri_send,
+    tri_recv,
+    left_f,
+    right_f,
+    tri_f,
+    proj_all,
+    out_all,
+    up_all,
+    down_all,
+    gain_all,
+    proj_t,
+    out_t,
+    up_t,
+    down_t,
+    gain_t,
+    pair_sem,
+    edge_send_sem,
+    edge_recv_sem,
+    tri_send_sem,
+    tri_recv_sem,
+    weight_send_sem,
+    weight_sem,
+):
+    section = lax.axis_index("section")
+    me = lax.axis_index("axial")
+    rows, width, channels = pair_buf.shape[1:]
+    per_group = channels // peers
+    lanes = sub_rows * width
+    steps = rows // sub_rows
+
+    pair_copies = []
+    for m in range(own_count):
+        copy = pltpu.make_async_copy(
+            pair_ref.at[section * own_count + m], pair_buf.at[m], pair_sem.at[m]
+        )
+        copy.start()
+        pair_copies.append(copy)
+
+    barrier = pltpu.get_barrier_semaphore()
+    for k in range(1, peers):
+        pl.semaphore_signal(
+            barrier, inc=1, device_id={"axial": lax.rem(me + k, peers)}, device_id_type=MESH
+        )
+    for k in range(1, sections):
+        pl.semaphore_signal(
+            barrier,
+            inc=1,
+            device_id={"section": lax.rem(section + k, sections)},
+            device_id_type=MESH,
+        )
+    pl.semaphore_wait(barrier, peers - 1 + sections - 1)
+
+    weights = (
+        (gain_ref, gain_all),
+        (proj_ref, proj_all),
+        (out_ref, out_all),
+        (up_ref, up_all),
+        (down_ref, down_all),
+    )
+    weight_copies = []
+    for a, (source, gathered) in enumerate(weights):
+        for k in range(1, sections):
+            copy = pltpu.make_async_remote_copy(
+                src_ref=source.at[0],
+                dst_ref=gathered.at[section],
+                send_sem=weight_send_sem.at[a, k],
+                recv_sem=weight_sem.at[a, section],
+                device_id={"section": lax.rem(section + k, sections)},
+                device_id_type=MESH,
+            )
+            copy.start()
+            weight_copies.append(copy)
+        pltpu.make_async_copy(source.at[0], gathered.at[section], weight_sem.at[a, section]).start()
+
+    def wait_weight(a, layer):
+        source, gathered = weights[a]
+        pltpu.make_async_copy(source.at[0], gathered.at[layer], weight_sem.at[a, layer]).wait()
+
+    def turned(values):
+        return values.astype(jnp.float32).T.astype(jnp.bfloat16)
+
+    def prepare_gains(layer):
+        wait_weight(0, layer)
+        for index in range(gain_t.shape[1]):
+            row = gain_all[layer, index : index + 1, :].astype(jnp.float32)
+            gain_t[layer, index] = jnp.broadcast_to(row, (width, channels)).T
+
+    def prepare_proj(layer):
+        wait_weight(1, layer)
+        for e in range(proj_t.shape[1]):
+            proj_t[layer, e] = turned(proj_all[layer, e])
+
+    def prepare_rest(layer):
+        for a in (2, 3, 4):
+            wait_weight(a, layer)
+        out_t[layer] = turned(out_all[layer])
+        up_t[layer] = turned(up_all[layer])
+        down_t[layer] = turned(down_all[layer])
+
+    def wide_gain(layer, index):
+        return jnp.concatenate([gain_t[layer, index]] * sub_rows, axis=1)
+
+    def load_pair(m):
+        pair_copies[m].wait()
+
+        def step(q, carry):
+            for s in range(sub_rows):
+                r = q * sub_rows + s
+                z_buf[m, q, :, s * width : (s + 1) * width] = pair_buf[m, r].astype(jnp.float32).T
+            return carry
+
+        lax.fori_loop(0, steps, step, 0)
+
+    def phase_norm(layer, m):
+        def step(q, carry):
+            normed_buf[m, q] = normalize_rows(z_buf[m, q], wide_gain(layer, 0)).astype(jnp.bfloat16)
+            return carry
+
+        lax.fori_loop(0, steps, step, 0)
+
+    def phase_edges(layer, m):
+        row_mask = mask_ref[pl.ds(section * own_count + m, 1), :].astype(jnp.float32)
+
+        def step(q, carry):
+            values = normed_buf[m, q]
+            masks = []
+            for s in range(sub_rows):
+                own = mask_smem[section * own_count + m, me * rows + q * sub_rows + s]
+                masks.append(row_mask * own.astype(jnp.float32))
+            pair_mask = jnp.concatenate(masks, axis=1)
+            for side in range(2):
+                value = matmul(proj_t[layer, 2 * side], values)
+                gate = matmul(proj_t[layer, 2 * side + 1], values)
+                edge = sigmoid(gate) * value * pair_mask
+                for s in range(sub_rows):
+                    part = edge[:, s * width : (s + 1) * width].reshape(peers, per_group, width)
+                    edge_send[m, :, side, q * sub_rows + s] = part.astype(jnp.bfloat16)
+            return carry
+
+        lax.fori_loop(0, steps, step, 0)
+
+    def phase_gate(layer, m):
+        def step(q, carry):
+            gate_buf[m, q] = sigmoid(matmul(proj_t[layer, 4], normed_buf[m, q]))
+            return carry
+
+        lax.fori_loop(0, steps, step, 0)
+
+    def edge_copy(m, peer):
+        return pltpu.make_async_remote_copy(
+            src_ref=edge_send.at[m, peer],
+            dst_ref=edge_recv.at[m, me],
+            send_sem=edge_send_sem.at[m, peer],
+            recv_sem=edge_recv_sem.at[m, me],
+            device_id={"axial": peer},
+            device_id_type=MESH,
+        )
+
+    def tri_copy(m, peer):
+        return pltpu.make_async_remote_copy(
+            src_ref=tri_send.at[m, peer],
+            dst_ref=tri_recv.at[m, me],
+            send_sem=tri_send_sem.at[m, peer],
+            recv_sem=tri_recv_sem.at[m, me],
+            device_id={"axial": peer},
+            device_id_type=MESH,
+        )
+
+    def send_all(make_copy, send, recv, recv_sem, m):
+        pltpu.make_async_copy(send.at[m, me], recv.at[m, me], recv_sem.at[m, me]).start()
+
+        def step(k, carry):
+            make_copy(m, lax.rem(me + k, peers)).start()
+            return carry
+
+        lax.fori_loop(1, peers, step, 0)
+
+    def wait_sent(make_copy, m):
+        def step(k, carry):
+            make_copy(m, lax.rem(me + k, peers)).wait_send()
+            return carry
+
+        lax.fori_loop(1, peers, step, 0)
+
+    def wait_all(send, recv, recv_sem, m):
+        def step(g, carry):
+            pltpu.make_async_copy(send.at[m, g], recv.at[m, g], recv_sem.at[m, g]).wait()
+            return carry
+
+        lax.fori_loop(0, peers, step, 0)
+
+    def phase_triangle(m):
+        for g in range(peers):
+            left_f[g * rows : (g + 1) * rows] = edge_recv[m, g, 0].astype(jnp.float32)
+            right_f[g * rows : (g + 1) * rows] = edge_recv[m, g, 1].astype(jnp.float32)
+        for c in range(per_group):
+            tri_f[:, c, :] = lax.dot_general(
+                left_f[:, c, :].astype(jnp.bfloat16),
+                right_f[:, c, :].astype(jnp.bfloat16),
+                (((1,), (1,)), ((), ())),
+                preferred_element_type=jnp.float32,
+            )
+        for g in range(peers):
+            tri_send[m, g] = tri_f[g * rows : (g + 1) * rows].astype(jnp.bfloat16)
+
+    def phase_update(layer, m, last):
+        def step(q, carry):
+            parts = []
+            for s in range(sub_rows):
+                part = tri_recv[m, :, q * sub_rows + s].astype(jnp.float32)
+                parts.append(part.reshape(channels, width))
+            tri = jnp.concatenate(parts, axis=1)
+            tri_norm = normalize_rows(tri, wide_gain(layer, 1)).astype(jnp.bfloat16)
+            mid = z_buf[m, q] + gate_buf[m, q] * matmul(out_t[layer], tri_norm)
+            trans_in = normalize_rows(mid, wide_gain(layer, 2)).astype(jnp.bfloat16)
+            hidden = jnp.maximum(matmul(up_t[layer], trans_in), 0.0).astype(jnp.bfloat16)
+            fresh = mid + matmul(down_t[layer], hidden)
+            if last:
+                for s in range(sub_rows):
+                    part = fresh[:, s * width : (s + 1) * width]
+                    result_ref[m, q * sub_rows + s] = part.T.astype(jnp.bfloat16)
+            else:
+                z_buf[m, q] = fresh.astype(jnp.bfloat16).astype(jnp.float32)
+            return carry
+
+        lax.fori_loop(0, steps, step, 0)
+
+    edges = (edge_copy, edge_send, edge_recv, edge_recv_sem)
+    tris = (tri_copy, tri_send, tri_recv, tri_recv_sem)
+    everyone = range(own_count)
+    for m in everyone:
+        load_pair(m)
+    prepare_gains(0)
+    for m in everyone:
+        phase_norm(0, m)
+    prepare_proj(0)
+    for m in everyone:
+        phase_edges(0, m)
+        send_all(*edges, m)
+    for m in everyone:
+        phase_gate(0, m)
+    prepare_rest(0)
+    for layer in range(1, sections):
+        prepare_gains(layer)
+        prepare_proj(layer)
+        prepare_rest(layer)
+    for layer in range(sections):
+        last = layer == sections - 1
+        for m in everyone:
+            wait_all(*edges[1:], m)
+            if layer > 0:
+                wait_sent(tri_copy, m)
+            phase_triangle(m)
+            send_all(*tris, m)
+        for m in everyone:
+            wait_all(*tris[1:], m)
+            phase_update(layer, m, last)
+            wait_sent(edge_copy, m)
+            if not last:
+                phase_norm(layer + 1, m)
+                phase_edges(layer + 1, m)
+                send_all(*edges, m)
+        if not last:
+            for m in everyone:
+                phase_gate(layer + 1, m)
+    for m in everyone:
+        wait_sent(tri_copy, m)
+    for copy in weight_copies:
+        copy.wait_send()
+
+
+def fused_device(pair_in, crop_mask, proj_weights, out_weights, up_weights, down_weights, norm_gains):
+    sections = lax.axis_size("section")
+    peers = lax.axis_size("axial")
+    micro_count, rows, width, channels = pair_in.shape
+    own_count = micro_count // sections
+    per_group = channels // peers
+    sub_rows = 2 if rows % 2 == 0 else 1
+    steps = rows // sub_rows
+    lanes = sub_rows * width
+    hidden = up_weights.shape[2]
+    gains = norm_gains.shape[1]
+    edge_kinds = proj_weights.shape[1]
+    bf16, f32 = jnp.bfloat16, jnp.float32
+    vmem = pl.BlockSpec(memory_space=pltpu.VMEM)
+    dma = pltpu.SemaphoreType.DMA
+    edge_shape = (own_count, peers, 2, rows, per_group, width)
+    tri_shape = (own_count, peers, rows, per_group, width)
+    wide_shape = (own_count, steps, channels, lanes)
+    channel_shape = (peers * rows, per_group, width)
+    return pl.pallas_call(
+        functools.partial(fused_kernel, sections, peers, own_count, sub_rows),
+        out_shape=jax.ShapeDtypeStruct((own_count, rows, width, channels), bf16),
+        in_specs=[pl.BlockSpec(memory_space=pl.ANY), vmem, pl.BlockSpec(memory_space=pltpu.SMEM)]
+        + [vmem] * 5,
+        out_specs=vmem,
+        scratch_shapes=[
+            pltpu.VMEM((own_count, rows, width, channels), bf16),
+            pltpu.VMEM(wide_shape, f32),
+            pltpu.VMEM(wide_shape, bf16),
+            pltpu.VMEM(wide_shape, f32),
+            pltpu.VMEM(edge_shape, bf16),
+            pltpu.VMEM(edge_shape, bf16),
+            pltpu.VMEM(tri_shape, bf16),
+            pltpu.VMEM(tri_shape, bf16),
+            pltpu.VMEM(channel_shape, f32),
+            pltpu.VMEM(channel_shape, f32),
+            pltpu.VMEM(channel_shape, f32),
+            pltpu.VMEM((sections,) + proj_weights.shape[1:], bf16),
+            pltpu.VMEM((sections,) + out_weights.shape[1:], bf16),
+            pltpu.VMEM((sections,) + up_weights.shape[1:], bf16),
+            pltpu.VMEM((sections,) + down_weights.shape[1:], bf16),
+            pltpu.VMEM((sections,) + norm_gains.shape[1:], bf16),
+            pltpu.VMEM((sections, edge_kinds, channels, channels), bf16),
+            pltpu.VMEM((sections, channels, channels), bf16),
+            pltpu.VMEM((sections, hidden, channels), bf16),
+            pltpu.VMEM((sections, channels, hidden), bf16),
+            pltpu.VMEM((sections, gains, channels, width), f32),
+            dma((own_count,)),
+            dma((own_count, peers)),
+            dma((own_count, peers)),
+            dma((own_count, peers)),
+            dma((own_count, peers)),
+            dma((5, sections)),
+            dma((5, sections)),
+        ],
+        compiler_params=pltpu.CompilerParams(
+            collective_id=0, has_side_effects=True, vmem_limit_bytes=48 * 1024 * 1024
+        ),
+    )(
+        pair_in,
+        crop_mask,
+        crop_mask,
+        proj_weights,
+        out_weights,
+        up_weights,
+        down_weights,
+        norm_gains,
+    )
+
+
+def fits_fused(pair_in):
+    channels, peers = pair_in.shape[3], lax.axis_size("axial")
+    whole_tiles = channels % (8 * peers) == 0 and pair_in.shape[1] % 8 == 0
+    return whole_tiles and pair_in.shape[2] % channels == 0
+
+
 def per_device(pair_in, crop_mask, proj_weights, out_weights, up_weights, down_weights, norm_gains):
+    if fits_fused(pair_in):
+        return fused_device(
+            pair_in, crop_mask, proj_weights, out_weights, up_weights, down_weights, norm_gains
+        )
     section_index = lax.axis_index("section")
     section_count = lax.axis_size("section")
     micro_count = pair_in.shape[0]

time: 209 us -> 96 us (0.46)
  Pallas kernels: 0 us -> 87.5 us
  waiting for transfers between devices: 69 us -> 0 us
  blocking collectives: 52.7 us -> 0 us
  starting transfers between devices: 42.8 us -> 0 us
  matrix products: 20.7 us -> 0 us
  other arithmetic: 13.6 us -> 0 us
    pallas_call x0 -> x1, Pallas kernels: none -> 87.5 us  [fused_device(): pl.pallas_call(functools.partial(fused_kernel, sections, peers, own_count...]
    all_to_all x10 -> x0, waiting for transfers between devices: 69 us -> none  [the longest x4 27.1 us: evo_block(): lax.all_to_all(right_groups, 'axial', split_axis=0, concat_axis=2, tiled=...]
    all_to_all x10 -> x0, starting transfers between devices: 42.8 us -> none  [the longest x4 17 us: evo_block(): lax.all_to_all(product, 'axial', split_axis=2, concat_axis=0, tiled=True)]
    all_gather x5 -> x0, blocking collectives: 27.3 us -> none  [the longest x1 6.47 us: per_device(): lax.all_gather(up_weights, 'section', axis=0, tiled=True)]
    all_to_all x2 -> x0, blocking collectives: 25.4 us -> none  [evo_block(): lax.all_to_all(left_groups, 'axial', split_axis=0, concat_axis=2, tiled=T...]
    dot_general x24 -> x0, matrix products: 20.7 us -> none  [the longest x4 5.75 us: evo_block(): jnp.einsum('rnd,dc->rnc', normed, proj_mats[4], preferred_element_type=jn...]
    unnamed x38 -> x15, local copies, waits for them, and re-layouts: 0.45 us -> 6.86 us
    reduce_sum x16 -> x0, other arithmetic: 6.23 us -> none  [the longest x11 4.44 us: normalize(): spread = jnp.mean(center * center, axis=axis_dim, keepdims=True)]
  transfers between devices with their start and end apart: 10 -> 0, of which waited for: 9 -> 0; matrix products, arithmetic and copies ran while one was open for 9% -> 0% of each run, Pallas kernels for 0% -> 0%
where the time goes in v1:
time: 96 us; the launch traced here: 94.4 us
  Pallas kernels  87.5 us (91%)
  local copies, waits for them, and re-layouts  6.86 us (7%)
    pallas_call x1, Pallas kernels, fused_device(): pl.pallas_call(functools.partial(fused_kernel, sections, peers, own_count...  87.5 us
    unnamed x15, local copies, waits for them, and re-layouts  6.86 us

profile of v1, /device:TPU:2, one launch (start us, length us, event | category | flops | bytes accessed | tf_op | source)
XLA Modules:
  0.0 94.4 jit_solution(9273841533830636351)
XLA Ops:
  0.0 0.0 copy-start
  0.0 1.2 %copy-done = bf16[4,8,128,128]{3,2,1,0:T(8,128)(2,1)S(1)} copy-done((bf16[4,8,128,128]{3,2,1,0:T(8,128)(2,1)S(1)}, bf16[4,8,128,128]{3,2,1,0:T(8,128)(2,1)}, u32[]{:S(2)}) %copy-start) | copy-done | bytes 1048600
  1.2 0.0 copy-start.1
  1.2 0.9 copy-done.1
  2.1 0.0 copy-start.2
  2.1 0.9 copy-done.2
  3.0 0.0 copy-start.3
  3.0 0.9 copy-done.3
  4.0 0.0 copy-start.4
  4.0 0.8 copy-done.4
  4.7 0.0 copy-start.5
  4.7 0.7 copy-done.5
  5.4 0.0 copy-start.6
  5.4 0.7 copy-done.6
  6.1 87.5 %shard_map.73 = bf16[2,8,128,128]{3,2,1,0:T(8,128)(2,1)S(1)} custom-call(bf16[4,8,128,128]{3,2,1,0:T(8,128)(2,1)S(1)} %copy-done, s32[4,128]{1,0:T(4,128)S(1)} %copy-done.5, s32[4,128]{1,0:T(4,128)S(1)} %copy-done.5, bf16[1,5,128,128]{3,2,1,0:T(8,128)(2,1)S(1)} %copy-done.1, bf16[1,128,128]{2,1,0:T(8,128)(2,1)S(1)} %copy-done.4, ...), custom_call_target="tpu_custom_call" | custom-call | tf_op jit(solution)/shard_map/pallas_call | solution.py:397
  93.6 0.8 copy.9
Async XLA Ops:
  0.0 1.2 %copy-start = (bf16[4,8,128,128]{3,2,1,0:T(8,128)(2,1)S(1)}, bf16[4,8,128,128]{3,2,1,0:T(8,128)(2,1)}, u32[]{:S(2)}) copy-start(bf16[4,8,128,128]{3,2,1,0:T(8,128)(2,1)} %pair_ref.1) | copy-start | bytes 3145732
  1.2 0.9 copy-start.1
  2.1 0.9 copy-start.2
  3.0 0.9 copy-start.3
  4.0 0.8 copy-start.4
  4.7 0.7 copy-start.5
  5.4 0.7 copy-start.6

commit v2 on v1

--- a/solution.py
+++ b/solution.py
@@ -87,6 +87,7 @@
 def fused_kernel(
     sections,
     peers,
+    halves,
     own_count,
     sub_rows,
     pair_ref,
@@ -103,7 +104,8 @@
     normed_buf,
     gate_buf,
     edge_send,
-    edge_recv,
+    left_recv,
+    right_recv,
     tri_send,
     tri_recv,
     left_f,
@@ -120,8 +122,10 @@
     down_t,
     gain_t,
     pair_sem,
-    edge_send_sem,
-    edge_recv_sem,
+    left_send_sem,
+    left_recv_sem,
+    right_send_sem,
+    right_recv_sem,
     tri_send_sem,
     tri_recv_sem,
     weight_send_sem,
@@ -130,8 +134,10 @@
     section = lax.axis_index("section")
     me = lax.axis_index("axial")
     rows, width, channels = pair_buf.shape[1:]
-    per_group = channels // peers
-    lanes = sub_rows * width
+    owners = peers // halves
+    per_group = channels // owners
+    my_half = me // owners
+    my_owner = lax.rem(me, owners)
     steps = rows // sub_rows
 
     pair_copies = []
@@ -239,7 +245,7 @@
                 gate = matmul(proj_t[layer, 2 * side + 1], values)
                 edge = sigmoid(gate) * value * pair_mask
                 for s in range(sub_rows):
-                    part = edge[:, s * width : (s + 1) * width].reshape(peers, per_group, width)
+                    part = edge[:, s * width : (s + 1) * width].reshape(owners, per_group, width)
                     edge_send[m, :, side, q * sub_rows + s] = part.astype(jnp.bfloat16)
             return carry
 
@@ -252,53 +258,92 @@
 
         lax.fori_loop(0, steps, step, 0)
 
-    def edge_copy(m, peer):
+    def left_copy(m, k):
+        owner = lax.rem(my_owner + k, owners)
         return pltpu.make_async_remote_copy(
-            src_ref=edge_send.at[m, peer],
-            dst_ref=edge_recv.at[m, me],
-            send_sem=edge_send_sem.at[m, peer],
-            recv_sem=edge_recv_sem.at[m, me],
-            device_id={"axial": peer},
+            src_ref=edge_send.at[m, owner, 0],
+            dst_ref=left_recv.at[m, my_owner],
+            send_sem=left_send_sem.at[m, k],
+            recv_sem=left_recv_sem.at[m, my_owner],
+            device_id={"axial": my_half * owners + owner},
             device_id_type=MESH,
         )
 
-    def tri_copy(m, peer):
+    def right_copy(slot, m, k):
+        half = lax.rem(my_half + k // owners, halves)
+        owner = lax.rem(my_owner + k % owners, owners)
         return pltpu.make_async_remote_copy(
-            src_ref=tri_send.at[m, peer],
-            dst_ref=tri_recv.at[m, me],
-            send_sem=tri_send_sem.at[m, peer],
-            recv_sem=tri_recv_sem.at[m, me],
-            device_id={"axial": peer},
+            src_ref=edge_send.at[m, owner, 1],
+            dst_ref=right_recv.at[slot, m, me],
+            send_sem=right_send_sem.at[m, k],
+            recv_sem=right_recv_sem.at[slot, m, me],
+            device_id={"axial": half * owners + owner},
             device_id_type=MESH,
         )
 
-    def send_all(make_copy, send, recv, recv_sem, m):
-        pltpu.make_async_copy(send.at[m, me], recv.at[m, me], recv_sem.at[m, me]).start()
-
-        def step(k, carry):
-            make_copy(m, lax.rem(me + k, peers)).start()
-            return carry
-
-        lax.fori_loop(1, peers, step, 0)
-
-    def wait_sent(make_copy, m):
-        def step(k, carry):
-            make_copy(m, lax.rem(me + k, peers)).wait_send()
-            return carry
-
-        lax.fori_loop(1, peers, step, 0)
-
-    def wait_all(send, recv, recv_sem, m):
-        def step(g, carry):
-            pltpu.make_async_copy(send.at[m, g], recv.at[m, g], recv_sem.at[m, g]).wait()
-            return carry
-
-        lax.fori_loop(0, peers, step, 0)
-
-    def phase_triangle(m):
+    def tri_copy(m, k):
+        owner = lax.rem(my_owner + k, owners)
+        return pltpu.make_async_remote_copy(
+            src_ref=tri_send.at[m, owner],
+            dst_ref=tri_recv.at[m, my_owner],
+            send_sem=tri_send_sem.at[m, k],
+            recv_sem=tri_recv_sem.at[m, my_owner],
+            device_id={"axial": my_half * owners + owner},
+            device_id_type=MESH,
+        )
+
+    def send_edges(slot, m):
+        pltpu.make_async_copy(
+            edge_send.at[m, my_owner, 0],
+            left_recv.at[m, my_owner],
+            left_recv_sem.at[m, my_owner],
+        ).start()
+        pltpu.make_async_copy(
+            edge_send.at[m, my_owner, 1],
+            right_recv.at[slot, m, me],
+            right_recv_sem.at[slot, m, me],
+        ).start()
+        for k in range(peers - 1, 0, -1):
+            right_copy(slot, m, k).start()
+        for k in range(owners - 1, 0, -1):
+            left_copy(m, k).start()
+
+    def wait_edges_sent(slot, m):
+        for k in range(1, peers):
+            right_copy(slot, m, k).wait_send()
+        for k in range(1, owners):
+            left_copy(m, k).wait_send()
+
+    def send_tri(m):
+        pltpu.make_async_copy(
+            tri_send.at[m, my_owner], tri_recv.at[m, my_owner], tri_recv_sem.at[m, my_owner]
+        ).start()
+        for k in range(owners - 1, 0, -1):
+            tri_copy(m, k).start()
+
+    def wait_tri_sent(m):
+        for k in range(1, owners):
+            tri_copy(m, k).wait_send()
+
+    def wait_left(m, g):
+        pltpu.make_async_copy(left_recv.at[m, g], left_recv.at[m, g], left_recv_sem.at[m, g]).wait()
+
+    def wait_right(slot, m, g):
+        pltpu.make_async_copy(
+            right_recv.at[slot, m, g], right_recv.at[slot, m, g], right_recv_sem.at[slot, m, g]
+        ).wait()
+
+    def wait_tri(m):
+        for g in range(owners):
+            pltpu.make_async_copy(tri_recv.at[m, g], tri_recv.at[m, g], tri_recv_sem.at[m, g]).wait()
+
+    def phase_triangle(slot, m):
+        for g in range(owners):
+            wait_left(m, g)
+            left_f[g * rows : (g + 1) * rows] = left_recv[m, g].astype(jnp.float32)
         for g in range(peers):
-            left_f[g * rows : (g + 1) * rows] = edge_recv[m, g, 0].astype(jnp.float32)
-            right_f[g * rows : (g + 1) * rows] = edge_recv[m, g, 1].astype(jnp.float32)
+            wait_right(slot, m, g)
+            right_f[g * rows : (g + 1) * rows] = right_recv[slot, m, g].astype(jnp.float32)
         for c in range(per_group):
             tri_f[:, c, :] = lax.dot_general(
                 left_f[:, c, :].astype(jnp.bfloat16),
@@ -306,7 +351,7 @@
                 (((1,), (1,)), ((), ())),
                 preferred_element_type=jnp.float32,
             )
-        for g in range(peers):
+        for g in range(owners):
             tri_send[m, g] = tri_f[g * rows : (g + 1) * rows].astype(jnp.bfloat16)
 
     def phase_update(layer, m, last):
@@ -331,8 +376,6 @@
 
         lax.fori_loop(0, steps, step, 0)
 
-    edges = (edge_copy, edge_send, edge_recv, edge_recv_sem)
-    tris = (tri_copy, tri_send, tri_recv, tri_recv_sem)
     everyone = range(own_count)
     for m in everyone:
         load_pair(m)
@@ -342,7 +385,7 @@
     prepare_proj(0)
     for m in everyone:
         phase_edges(0, m)
-        send_all(*edges, m)
+        send_edges(0, m)
     for m in everyone:
         phase_gate(0, m)
     prepare_rest(0)
@@ -353,24 +396,23 @@
     for layer in range(sections):
         last = layer == sections - 1
         for m in everyone:
-            wait_all(*edges[1:], m)
             if layer > 0:
-                wait_sent(tri_copy, m)
-            phase_triangle(m)
-            send_all(*tris, m)
+                wait_tri_sent(m)
+            phase_triangle(layer % 2, m)
+            send_tri(m)
         for m in everyone:
-            wait_all(*tris[1:], m)
+            wait_tri(m)
             phase_update(layer, m, last)
-            wait_sent(edge_copy, m)
+            wait_edges_sent(layer % 2, m)
             if not last:
                 phase_norm(layer + 1, m)
                 phase_edges(layer + 1, m)
-                send_all(*edges, m)
+                send_edges((layer + 1) % 2, m)
         if not last:
             for m in everyone:
                 phase_gate(layer + 1, m)
     for m in everyone:
-        wait_sent(tri_copy, m)
+        wait_tri_sent(m)
     for copy in weight_copies:
         copy.wait_send()
 
@@ -380,7 +422,9 @@
     peers = lax.axis_size("axial")
     micro_count, rows, width, channels = pair_in.shape
     own_count = micro_count // sections
-    per_group = channels // peers
+    halves = half_count(pair_in)
+    owners = peers // halves
+    per_group = channels // owners
     sub_rows = 2 if rows % 2 == 0 else 1
     steps = rows // sub_rows
     lanes = sub_rows * width
@@ -389,16 +433,16 @@
     edge_kinds = proj_weights.shape[1]
     bf16, f32 = jnp.bfloat16, jnp.float32
     vmem = pl.BlockSpec(memory_space=pltpu.VMEM)
+    hbm = pl.BlockSpec(memory_space=pltpu.HBM)
     dma = pltpu.SemaphoreType.DMA
-    edge_shape = (own_count, peers, 2, rows, per_group, width)
-    tri_shape = (own_count, peers, rows, per_group, width)
+    edge_shape = (own_count, owners, 2, rows, per_group, width)
+    left_shape = (own_count, owners, rows, per_group, width)
+    right_shape = (2, own_count, peers, rows, per_group, width)
     wide_shape = (own_count, steps, channels, lanes)
-    channel_shape = (peers * rows, per_group, width)
     return pl.pallas_call(
-        functools.partial(fused_kernel, sections, peers, own_count, sub_rows),
+        functools.partial(fused_kernel, sections, peers, halves, own_count, sub_rows),
         out_shape=jax.ShapeDtypeStruct((own_count, rows, width, channels), bf16),
-        in_specs=[pl.BlockSpec(memory_space=pl.ANY), vmem, pl.BlockSpec(memory_space=pltpu.SMEM)]
-        + [vmem] * 5,
+        in_specs=[hbm, vmem, pl.BlockSpec(memory_space=pltpu.SMEM)] + [hbm] * 5,
         out_specs=vmem,
         scratch_shapes=[
             pltpu.VMEM((own_count, rows, width, channels), bf16),
@@ -406,12 +450,13 @@
             pltpu.VMEM(wide_shape, bf16),
             pltpu.VMEM(wide_shape, f32),
             pltpu.VMEM(edge_shape, bf16),
-            pltpu.VMEM(edge_shape, bf16),
-            pltpu.VMEM(tri_shape, bf16),
-            pltpu.VMEM(tri_shape, bf16),
-            pltpu.VMEM(channel_shape, f32),
-            pltpu.VMEM(channel_shape, f32),
-            pltpu.VMEM(channel_shape, f32),
+            pltpu.VMEM(left_shape, bf16),
+            pltpu.VMEM(right_shape, bf16),
+            pltpu.VMEM(left_shape, bf16),
+            pltpu.VMEM(left_shape, bf16),
+            pltpu.VMEM((owners * rows, per_group, width), f32),
+            pltpu.VMEM((peers * rows, per_group, width), f32),
+            pltpu.VMEM((owners * rows, per_group, width), f32),
             pltpu.VMEM((sections,) + proj_weights.shape[1:], bf16),
             pltpu.VMEM((sections,) + out_weights.shape[1:], bf16),
             pltpu.VMEM((sections,) + up_weights.shape[1:], bf16),
@@ -423,15 +468,17 @@
             pltpu.VMEM((sections, channels, hidden), bf16),
             pltpu.VMEM((sections, gains, channels, width), f32),
             dma((own_count,)),
+            dma((own_count, owners)),
+            dma((own_count, owners)),
             dma((own_count, peers)),
-            dma((own_count, peers)),
-            dma((own_count, peers)),
-            dma((own_count, peers)),
+            dma((2, own_count, peers)),
+            dma((own_count, owners)),
+            dma((own_count, owners)),
             dma((5, sections)),
             dma((5, sections)),
         ],
         compiler_params=pltpu.CompilerParams(
-            collective_id=0, has_side_effects=True, vmem_limit_bytes=48 * 1024 * 1024
+            collective_id=0, has_side_effects=True, vmem_limit_bytes=67043328
         ),
     )(
         pair_in,
@@ -445,10 +492,15 @@
     )
 
 
+def half_count(pair_in):
+    peers = lax.axis_size("axial")
+    return 2 if peers % 2 == 0 and pair_in.shape[3] % (8 * (peers // 2)) == 0 else 1
+
+
 def fits_fused(pair_in):
-    channels, peers = pair_in.shape[3], lax.axis_size("axial")
-    whole_tiles = channels % (8 * peers) == 0 and pair_in.shape[1] % 8 == 0
-    return whole_tiles and pair_in.shape[2] % channels == 0
+    rows, width, channels = pair_in.shape[1:]
+    owners = lax.axis_size("axial") // half_count(pair_in)
+    return channels % (8 * owners) == 0 and rows % 8 == 0 and width % 128 == 0
 
 
 def per_device(pair_in, crop_mask, proj_weights, out_weights, up_weights, down_weights, norm_gains):

time: 96 us -> 81.5 us (0.85); the launches traced: 94.4 us -> 81.3 us
  Pallas kernels: 87.5 us -> 79.4 us
  local copies, waits for them, and re-layouts: 6.86 us -> 1.89 us
    pallas_call x1, Pallas kernels: 87.5 us -> 79.4 us  [fused_device(): pl.pallas_call(functools.partial(fused_kernel, sections, peers, halves, o...]
    unnamed x15 -> x1, local copies, waits for them, and re-layouts: 6.86 us -> 1.89 us
where the time goes in v2:
time: 81.5 us; the launch traced here: 81.3 us
  Pallas kernels  79.4 us (97%)
  local copies, waits for them, and re-layouts  1.89 us (2%)
    pallas_call x1, Pallas kernels, fused_device(): pl.pallas_call(functools.partial(fused_kernel, sections, peers, halves, o...  79.4 us
    unnamed x1, local copies, waits for them, and re-layouts  1.89 us

profile of v2, /device:TPU:2, one launch (start us, length us, event | category | flops | bytes accessed | tf_op | source)
XLA Modules:
  0.0 81.3 jit_solution(17295215024824822371)
XLA Ops:
  0.0 79.4 %shard_map.73 = bf16[2,8,128,128]{3,2,1,0:T(8,128)(2,1)} custom-call(bf16[4,8,128,128]{3,2,1,0:T(8,128)(2,1)} %pair_ref.1, s32[4,128]{1,0:T(4,128)} %mask_smem.1, s32[4,128]{1,0:T(4,128)} %mask_smem.1, bf16[1,5,128,128]{3,2,1,0:T(8,128)(2,1)} %proj_ref.1, bf16[1,128,128]{2,1,0:T(8,128)(2,1)} %out_ref.1, bf16[1,128,512]{2,1,0:T(8,128)(2,1)} %up_ref.1, ...), custom_call_target="tpu_custom_call" | custom-call | tf_op jit(solution)/shard_map/pallas_call | solution.py:442
  79.4 1.9 %copy.9 = bf16[2,8,128,128]{3,2,1,0:T(8,128)(2,1)} copy(bf16[2,8,128,128]{3,2,1,0:T(8,128)(2,1)} %shard_map.73) | data formatting | bytes 1048576

commit v3 on v2

--- a/solution.py
+++ b/solution.py
@@ -160,33 +160,45 @@
             device_id={"section": lax.rem(section + k, sections)},
             device_id_type=MESH,
         )
-    pl.semaphore_wait(barrier, peers - 1 + sections - 1)
-
     weights = (
-        (gain_ref, gain_all),
-        (proj_ref, proj_all),
-        (out_ref, out_all),
-        (up_ref, up_all),
-        (down_ref, down_all),
-    )
-    weight_copies = []
-    for a, (source, gathered) in enumerate(weights):
-        for k in range(1, sections):
-            copy = pltpu.make_async_remote_copy(
-                src_ref=source.at[0],
-                dst_ref=gathered.at[section],
-                send_sem=weight_send_sem.at[a, k],
-                recv_sem=weight_sem.at[a, section],
-                device_id={"section": lax.rem(section + k, sections)},
-                device_id_type=MESH,
-            )
-            copy.start()
-            weight_copies.append(copy)
-        pltpu.make_async_copy(source.at[0], gathered.at[section], weight_sem.at[a, section]).start()
+        (gain_ref, gain_all, None),
+        (proj_ref, proj_all, (2, 2)),
+        (proj_ref, proj_all, (0, 2)),
+        (proj_ref, proj_all, (4, 1)),
+        (out_ref, out_all, None),
+        (up_ref, up_all, None),
+        (down_ref, down_all, None),
+    )
+
+    def weight_part(ref, layer, span):
+        return ref.at[layer] if span is None else ref.at[layer, pl.ds(*span)]
+
+    for a, (source, gathered, span) in enumerate(weights):
+        pltpu.make_async_copy(
+            weight_part(source, 0, span),
+            weight_part(gathered, section, span),
+            weight_sem.at[a, section],
+        ).start()
+
+    def send_weights():
+        copies = []
+        for a, (_, gathered, span) in enumerate(weights):
+            for k in range(1, sections):
+                copy = pltpu.make_async_remote_copy(
+                    src_ref=weight_part(gathered, section, span),
+                    dst_ref=weight_part(gathered, section, span),
+                    send_sem=weight_send_sem.at[a, k],
+                    recv_sem=weight_sem.at[a, section],
+                    device_id={"section": lax.rem(section + k, sections)},
+                    device_id_type=MESH,
+                )
+                copy.start()
+                copies.append(copy)
+        return copies
 
     def wait_weight(a, layer):
-        source, gathered = weights[a]
-        pltpu.make_async_copy(source.at[0], gathered.at[layer], weight_sem.at[a, layer]).wait()
+        part = weight_part(weights[a][1], layer, weights[a][2])
+        pltpu.make_async_copy(part, part, weight_sem.at[a, layer]).wait()
 
     def turned(values):
         return values.astype(jnp.float32).T.astype(jnp.bfloat16)
@@ -197,17 +209,25 @@
             row = gain_all[layer, index : index + 1, :].astype(jnp.float32)
             gain_t[layer, index] = jnp.broadcast_to(row, (width, channels)).T
 
-    def prepare_proj(layer):
-        wait_weight(1, layer)
-        for e in range(proj_t.shape[1]):
+    def prepare_proj(layer, side):
+        wait_weight(2 - side, layer)
+        for e in (2 * side, 2 * side + 1):
             proj_t[layer, e] = turned(proj_all[layer, e])
 
     def prepare_rest(layer):
-        for a in (2, 3, 4):
+        wait_weight(3, layer)
+        proj_t[layer, 4] = turned(proj_all[layer, 4])
+        for a in (4, 5, 6):
             wait_weight(a, layer)
         out_t[layer] = turned(out_all[layer])
         up_t[layer] = turned(up_all[layer])
         down_t[layer] = turned(down_all[layer])
+
+    def prepare_all(layer):
+        prepare_gains(layer)
+        prepare_proj(layer, 1)
+        prepare_proj(layer, 0)
+        prepare_rest(layer)
 
     def wide_gain(layer, index):
         return jnp.concatenate([gain_t[layer, index]] * sub_rows, axis=1)
@@ -221,16 +241,16 @@
                 z_buf[m, q, :, s * width : (s + 1) * width] = pair_buf[m, r].astype(jnp.float32).T
             return carry
 
-        lax.fori_loop(0, steps, step, 0)
+        lax.fori_loop(0, steps, step, 0, unroll=True)
 
     def phase_norm(layer, m):
         def step(q, carry):
             normed_buf[m, q] = normalize_rows(z_buf[m, q], wide_gain(layer, 0)).astype(jnp.bfloat16)
             return carry
 
-        lax.fori_loop(0, steps, step, 0)
-
-    def phase_edges(layer, m):
+        lax.fori_loop(0, steps, step, 0, unroll=True)
+
+    def phase_edges(layer, m, side):
         row_mask = mask_ref[pl.ds(section * own_count + m, 1), :].astype(jnp.float32)
 
         def step(q, carry):
@@ -240,23 +260,22 @@
                 own = mask_smem[section * own_count + m, me * rows + q * sub_rows + s]
                 masks.append(row_mask * own.astype(jnp.float32))
             pair_mask = jnp.concatenate(masks, axis=1)
-            for side in range(2):
-                value = matmul(proj_t[layer, 2 * side], values)
-                gate = matmul(proj_t[layer, 2 * side + 1], values)
-                edge = sigmoid(gate) * value * pair_mask
-                for s in range(sub_rows):
-                    part = edge[:, s * width : (s + 1) * width].reshape(owners, per_group, width)
-                    edge_send[m, :, side, q * sub_rows + s] = part.astype(jnp.bfloat16)
+            value = matmul(proj_t[layer, 2 * side], values)
+            gate = matmul(proj_t[layer, 2 * side + 1], values)
+            edge = sigmoid(gate) * value * pair_mask
+            for s in range(sub_rows):
+                part = edge[:, s * width : (s + 1) * width].reshape(owners, per_group, width)
+                edge_send[m, :, side, q * sub_rows + s] = part.astype(jnp.bfloat16)
             return carry
 
-        lax.fori_loop(0, steps, step, 0)
+        lax.fori_loop(0, steps, step, 0, unroll=True)
 
     def phase_gate(layer, m):
         def step(q, carry):
             gate_buf[m, q] = sigmoid(matmul(proj_t[layer, 4], normed_buf[m, q]))
             return carry
 
-        lax.fori_loop(0, steps, step, 0)
+        lax.fori_loop(0, steps, step, 0, unroll=True)
 
     def left_copy(m, k):
         owner = lax.rem(my_owner + k, owners)
@@ -292,12 +311,7 @@
             device_id_type=MESH,
         )
 
-    def send_edges(slot, m):
-        pltpu.make_async_copy(
-            edge_send.at[m, my_owner, 0],
-            left_recv.at[m, my_owner],
-            left_recv_sem.at[m, my_owner],
-        ).start()
+    def send_right(slot, m):
         pltpu.make_async_copy(
             edge_send.at[m, my_owner, 1],
             right_recv.at[slot, m, me],
@@ -305,6 +319,13 @@
         ).start()
         for k in range(peers - 1, 0, -1):
             right_copy(slot, m, k).start()
+
+    def send_left(m):
+        pltpu.make_async_copy(
+            edge_send.at[m, my_owner, 0],
+            left_recv.at[m, my_owner],
+            left_recv_sem.at[m, my_owner],
+        ).start()
         for k in range(owners - 1, 0, -1):
             left_copy(m, k).start()
 
@@ -374,25 +395,56 @@
                 z_buf[m, q] = fresh.astype(jnp.bfloat16).astype(jnp.float32)
             return carry
 
-        lax.fori_loop(0, steps, step, 0)
+        lax.fori_loop(0, steps, step, 0, unroll=True)
 
     everyone = range(own_count)
     for m in everyone:
         load_pair(m)
-    prepare_gains(0)
+    prepare_all(section)
+
+    @pl.when(section == 0)
+    def early_edges():
+        for m in everyone:
+            phase_norm(0, m)
+            phase_edges(0, m, 1)
+            phase_edges(0, m, 0)
+
+    pl.semaphore_wait(barrier, peers - 1 + sections - 1)
+    weight_copies = send_weights()
+
+    @pl.when(section != 0)
+    def late_norm():
+        prepare_gains(0)
+        for m in everyone:
+            phase_norm(0, m)
+
     for m in everyone:
-        phase_norm(0, m)
-    prepare_proj(0)
-    for m in everyone:
-        phase_edges(0, m)
-        send_edges(0, m)
+        for side in (1, 0):
+
+            @pl.when(section != 0)
+            def late_edges():
+                if m == 0:
+                    prepare_proj(0, side)
+                phase_edges(0, m, side)
+
+            if side:
+                send_right(0, m)
+            else:
+                send_left(m)
+
+    @pl.when(section != 0)
+    def late_rest():
+        prepare_rest(0)
+
     for m in everyone:
         phase_gate(0, m)
-    prepare_rest(0)
+
     for layer in range(1, sections):
-        prepare_gains(layer)
-        prepare_proj(layer)
-        prepare_rest(layer)
+
+        @pl.when(section != layer)
+        def other_weights():
+            prepare_all(layer)
+
     for layer in range(sections):
         last = layer == sections - 1
         for m in everyone:
@@ -406,8 +458,10 @@
             wait_edges_sent(layer % 2, m)
             if not last:
                 phase_norm(layer + 1, m)
-                phase_edges(layer + 1, m)
-                send_edges((layer + 1) % 2, m)
+                phase_edges(layer + 1, m, 1)
+                send_right((layer + 1) % 2, m)
+                phase_edges(layer + 1, m, 0)
+                send_left(m)
         if not last:
             for m in everyone:
                 phase_gate(layer + 1, m)
@@ -474,8 +528,8 @@
             dma((2, own_count, peers)),
             dma((own_count, owners)),
             dma((own_count, owners)),
-            dma((5, sections)),
-            dma((5, sections)),
+            dma((7, sections)),
+            dma((7, sections)),
         ],
         compiler_params=pltpu.CompilerParams(
             collective_id=0, has_side_effects=True, vmem_limit_bytes=67043328

time: 81.5 us -> 76.6 us (0.940)
  Pallas kernels: 79.4 us -> 74.5 us
    pallas_call x1, Pallas kernels: 79.4 us -> 74.5 us  [fused_device(): pl.pallas_call(functools.partial(fused_kernel, sections, peers, halves, o...]
where the time goes in v3:
time: 76.6 us; the launch traced here: 76.4 us
  Pallas kernels  74.5 us (97%)
  local copies, waits for them, and re-layouts  1.89 us (2%)
    pallas_call x1, Pallas kernels, fused_device(): pl.pallas_call(functools.partial(fused_kernel, sections, peers, halves, o...  74.5 us
    unnamed x1, local copies, waits for them, and re-layouts  1.89 us

profile of v3, /device:TPU:2, one launch (start us, length us, event | category | flops | bytes accessed | tf_op | source)
XLA Modules:
  0.0 76.4 jit_solution(15380271723972875382)
XLA Ops:
  0.0 74.5 %shard_map.73 = bf16[2,8,128,128]{3,2,1,0:T(8,128)(2,1)} custom-call(bf16[4,8,128,128]{3,2,1,0:T(8,128)(2,1)} %pair_ref.1, s32[4,128]{1,0:T(4,128)} %mask_smem.1, s32[4,128]{1,0:T(4,128)} %mask_smem.1, bf16[1,5,128,128]{3,2,1,0:T(8,128)(2,1)} %proj_ref.1, bf16[1,128,128]{2,1,0:T(8,128)(2,1)} %out_ref.1, bf16[1,128,512]{2,1,0:T(8,128)(2,1)} %up_ref.1, ...), custom_call_target="tpu_custom_call" | custom-call | tf_op jit(solution)/shard_map/pallas_call | solution.py:496
  74.5 1.9 %copy.9 = bf16[2,8,128,128]{3,2,1,0:T(8,128)(2,1)} copy(bf16[2,8,128,128]{3,2,1,0:T(8,128)(2,1)} %shard_map.73) | data formatting | bytes 1048576
